TPU v7x, 32 devices: a whole 2x2x4 slice. The times are simulated.
32 devices in a mesh: mod: 2 (over y), exp: 16 (over z, x, core).
Axes of the slice: x: 2, y: 2, z: 4, core: 2. Of those that a mesh axis runs over, the one named last changes fastest.
Arguments:
- tokens: bfloat16 [2, 8192, 1024], P('mod', 'exp'), may hold values from -60 to 60
- bottleneck: bfloat16 [64, 4, 1024], P('exp'), may hold values from -6 to 6
- clip_ids: int32 [2, 8192], P('mod', 'exp'), may hold values from 0 to 63, as said below
- expert_ids: int32 [2, 8192], P('mod', 'exp'), may hold values from 0 to 15, as said below
- slots: int32 [2, 8192], P('mod', 'exp'), may hold values from 0 to 127, as said below
- norm1_gain: bfloat16 [2, 1024], P('mod'), may hold values from 0.099609375 to 1.8984375
- attn_qkv: bfloat16 [2, 1024, 3072], P('mod'), may hold values from -2 to 2
- attn_out: bfloat16 [2, 1024, 1024], P('mod'), may hold values from -0.1875 to 0.1875
- norm2_gain: bfloat16 [2, 1024], P('mod'), may hold values from 0.099609375 to 1.8984375
- router: bfloat16 [1024, 16], replicated, may hold values from -0.1875 to 0.1875
- fc_in: bfloat16 [16, 1024, 4096], P('exp'), may hold values from -0.1875 to 0.1875
- fc_out: bfloat16 [16, 4096, 1024], P('exp'), may hold values from -0.09375 to 0.09375
Outputs:
- mixed_tokens: bfloat16 [2, 8192, 1024], P('mod', 'exp')
- new_bottleneck: bfloat16 [64, 4, 1024], P('exp')
Inputs may be any that keep to these rules, and one draw needn't show every extreme that they name: `clip_ids`: Non-decreasing in each modality; the tokens of block b of 512 rows belong to clips b * 4 to (b + 1) * 4 - 1, each of which has one or more of them. `expert_ids`: each token's single expert. For the k tokens of one block of 512 rows of one modality that share an expert, the slots are 0 to k - 1 in some order; k is at most 128; in every block of each modality one expert, the same for all blocks of that modality, has k = 128.
All inputs are finite; a program needn't handle non-finite values.
Results may differ from a plain program's by a relative error of at most 0.0085.
Values may be sent and summed in bfloat16 or wider, within the bound.
A program may use at most 128 MiB of HBM per device.

v0:
```python
import functools
import math

import jax
import jax.numpy as jnp
from jax import lax
from jax.experimental import pallas as pl
from jax.experimental.pallas import tpu as pltpu
from jax.sharding import PartitionSpec as P

MESH = pl.DeviceIdType.MESH
HEAD = 64
CAP_FACTOR = 2


EPSILON = 1e-06


def layer_norm(features, scales):
    row_mean = jnp.mean(features, axis=-1, keepdims=True)
    centred = features - row_mean
    spread = jnp.mean(centred * centred, axis=-1, keepdims=True)
    return centred * lax.rsqrt(spread + EPSILON) * scales.astype(jnp.float32)


def attention_kernel(pair, rows_ref, cols_ref, q_ref, k_ref, v_ref, out_ref):
    allowed = rows_ref[...] == cols_ref[...]
    lane = lax.broadcasted_iota(jnp.int32, q_ref.shape, 1) // HEAD
    queries = q_ref[...] * jnp.bfloat16(1.0 / math.sqrt(HEAD))
    attended = jnp.zeros(out_ref.shape, jnp.float32)
    for head in range(pair):
        mine = lane == head
        scores = lax.dot_general(
            jnp.where(mine, queries, jnp.zeros_like(queries)),
            k_ref[...],
            (((1,), (1,)), ((), ())),
            preferred_element_type=jnp.float32,
        )
        scores = jnp.where(allowed, scores, -jnp.inf)
        weights = jnp.exp(scores - jnp.max(scores, axis=-1, keepdims=True))
        total = jnp.sum(weights, axis=-1, keepdims=True)
        summed = jnp.dot(
            weights.astype(jnp.bfloat16), v_ref[...], preferred_element_type=jnp.float32
        )
        attended = jnp.where(mine, summed / total, attended)
    out_ref[...] = attended.astype(jnp.bfloat16)


def attention(packed, row_clip):
    rows, width = packed.shape[0], packed.shape[1] // 3
    pair = 128 // HEAD
    steps = width // 128

    def part(index):
        return pl.BlockSpec((rows, 128), lambda step: (0, index * steps + step))

    return pl.pallas_call(
        functools.partial(attention_kernel, pair),
        grid=(steps,),
        out_shape=jax.ShapeDtypeStruct((rows, width), jnp.bfloat16),
        in_specs=[
            pl.BlockSpec((rows, 1), lambda step: (0, 0)),
            pl.BlockSpec((1, rows), lambda step: (0, 0)),
            part(0),
            part(1),
            part(2),
        ],
        out_specs=pl.BlockSpec((rows, 128), lambda step: (0, step)),
        compiler_params=pltpu.CompilerParams(vmem_limit_bytes=32 * 1024 * 1024),
    )(row_clip[:, None], row_clip[None, :], packed, packed, packed)


def attend(token_rows, latent_rows, token_clip, clip_start, scales, w_qkv, w_out):
    n_clips, n_latent, model_width = latent_rows.shape
    n_tokens = token_rows.shape[0]
    all_rows = jnp.concatenate(
        [token_rows, latent_rows.reshape(n_clips * n_latent, model_width)], axis=0
    )
    row_count = all_rows.shape[0]
    normed = layer_norm(all_rows.astype(jnp.float32), scales).astype(jnp.bfloat16)
    packed = jnp.dot(normed, w_qkv, preferred_element_type=jnp.float32).astype(jnp.bfloat16)
    latent_clip = clip_start + jnp.arange(n_clips * n_latent, dtype=jnp.int32) // n_latent
    row_clip = jnp.concatenate([token_clip, latent_clip])
    attended = attention(packed, row_clip)
    updated = all_rows.astype(jnp.float32) + jnp.dot(
        attended, w_out, preferred_element_type=jnp.float32
    )
    return (updated[:n_tokens], updated[n_tokens:].reshape(n_clips, n_latent, model_width))


def gelu(x):
    half = 0.5 * x
    return half + half * lax.erf(x * (1.0 / math.sqrt(2.0)))


def near_count(size):
    return 4 if size % 4 == 0 else 1


def moe_kernel(
    size,
    cap,
    tile,
    latent_ref,
    buf_ref,
    w_in_hbm,
    w_out_hbm,
    out_ref,
    mean_ref,
    w_in,
    w_out,
    recv,
    res,
    acc,
    act,
    peer_latent,
    w_sems,
    own_sems,
    lat_sems,
    send_sems,
    recv_sems,
    back_send,
    back_recv,
):
    near = near_count(size)
    far = size // near
    me = lax.axis_index("exp")
    mod = lax.axis_index("mod")
    high, low = me // near, me % near
    shifts = [0] + sorted(range(1, far), key=lambda s: (abs(2 * s - far), s))
    order = [(s, d) for s in shifts for d in range(near)]

    def ahead(step):
        s, d = order[step]
        return ((high + s) % far) * near + (low + d) % near

    def behind(step):
        s, d = order[step]
        return ((high + far - s) % far) * near + (low + near - d) % near

    def block(index):
        return pl.ds(pl.multiple_of(index * cap, cap), cap)

    load_in = pltpu.make_async_copy(w_in_hbm, w_in, w_sems.at[0])
    load_out = pltpu.make_async_copy(w_out_hbm, w_out, w_sems.at[1])
    load_in.start()
    load_out.start()

    barrier = pltpu.get_barrier_semaphore()
    for step in range(1, size):
        pl.semaphore_signal(barrier, inc=1, device_id=(mod, ahead(step)), device_id_type=MESH)
    pl.semaphore_signal(barrier, inc=1, device_id=(1 - mod, me), device_id_type=MESH)
    pl.semaphore_wait(barrier, size)

    sends = [None]
    for step in range(1, size):
        sends.append(
            pltpu.make_async_remote_copy(
                src_ref=buf_ref.at[block(ahead(step))],
                dst_ref=recv.at[pl.ds(step * cap, cap)],
                send_sem=send_sems.at[step],
                recv_sem=recv_sems.at[step],
                device_id=(mod, ahead(step)),
                device_id_type=MESH,
            )
        )
    backs = [None]
    for step in range(1, size):
        backs.append(
            pltpu.make_async_remote_copy(
                src_ref=res.at[pl.ds(step * cap, cap)],
                dst_ref=out_ref.at[block(me)],
                send_sem=back_send.at[step],
                recv_sem=back_recv.at[step],
                device_id=(mod, behind(step)),
                device_id_type=MESH,
            )
        )
    for step in range(1, size):
        sends[step].start()
    latent_copy = pltpu.make_async_remote_copy(
        src_ref=latent_ref,
        dst_ref=peer_latent,
        send_sem=lat_sems.at[0],
        recv_sem=lat_sems.at[1],
        device_id=(1 - mod, me),
        device_id_type=MESH,
    )
    latent_copy.start()
    own = pltpu.make_async_copy(buf_ref.at[block(me)], recv.at[pl.ds(0, cap)], own_sems.at[0])
    own.start()
    own.wait()

    groups = 2 if size % 4 == 0 else 1
    per = size // groups
    rows = per * cap
    tiles = w_in.shape[1] // tile
    own_back = pltpu.make_async_copy(res.at[pl.ds(0, cap)], out_ref.at[block(me)], own_sems.at[1])
    for g in range(groups):
        for step in range(g * per, (g + 1) * per):
            if step:
                sends[step].wait_recv()
        if g == 0:
            load_in.wait()
            load_out.wait()
        here = pl.ds(g * rows, rows)

        def hidden(t):
            cols = pl.ds(pl.multiple_of(t * tile, tile), tile)
            return gelu(
                jnp.dot(recv[here, :], w_in[:, cols], preferred_element_type=jnp.float32)
            ).astype(jnp.bfloat16)

        def project(t, slot):
            cols = pl.ds(pl.multiple_of(t * tile, tile), tile)
            return jnp.dot(act[slot], w_out[cols, :], preferred_element_type=jnp.float32)

        act[0] = hidden(0)
        acc[...] = jnp.zeros_like(acc)

        def body(t, carry):
            acc[...] += project(t - 1, (t + 1) % 2)
            act[t % 2] = hidden(t)
            return carry

        lax.fori_loop(1, tiles, body, 0)
        res[here, :] = (acc[...] + project(tiles - 1, (tiles - 1) % 2)).astype(jnp.bfloat16)
        for step in range(g * per, (g + 1) * per):
            if step:
                backs[step].start()
            else:
                own_back.start()

    latent_copy.wait()
    mean_ref[...] = ((latent_ref[...] + peer_latent[...]) * 0.5).astype(jnp.bfloat16)
    own_back.wait()
    for step in range(1, size):
        sends[step].wait_send()
        backs[step].wait()


def exchange_experts(mid_latent, buffer, weight_in, weight_out, size):
    rows, width = buffer.shape
    cap = rows // size
    hidden_width = weight_in.shape[1]
    tile = 1024
    groups = 2 if size % 4 == 0 else 1
    vmem = pl.BlockSpec(memory_space=pltpu.VMEM)
    hbm = pl.BlockSpec(memory_space=pl.ANY)
    return pl.pallas_call(
        functools.partial(moe_kernel, size, cap, tile),
        out_shape=(
            jax.ShapeDtypeStruct((rows, width), jnp.bfloat16),
            jax.ShapeDtypeStruct(mid_latent.shape, jnp.bfloat16),
        ),
        in_specs=[vmem, vmem, hbm, hbm],
        out_specs=(vmem, vmem),
        scratch_shapes=[
            pltpu.VMEM((width, hidden_width), jnp.bfloat16),
            pltpu.VMEM((hidden_width, width), jnp.bfloat16),
            pltpu.VMEM((rows, width), jnp.bfloat16),
            pltpu.VMEM((rows, width), jnp.bfloat16),
            pltpu.VMEM((rows // groups, width), jnp.float32),
            pltpu.VMEM((2, rows // groups, tile), jnp.bfloat16),
            pltpu.VMEM(mid_latent.shape, jnp.float32),
            pltpu.SemaphoreType.DMA((2,)),
            pltpu.SemaphoreType.DMA((2,)),
            pltpu.SemaphoreType.DMA((2,)),
            pltpu.SemaphoreType.DMA((size,)),
            pltpu.SemaphoreType.DMA((size,)),
            pltpu.SemaphoreType.DMA((size,)),
            pltpu.SemaphoreType.DMA((size,)),
        ],
        compiler_params=pltpu.CompilerParams(
            collective_id=0, has_side_effects=True, vmem_limit_bytes=48 * 1024 * 1024
        ),
    )(mid_latent, buffer, weight_in, weight_out)


def mixture(mid_tokens, mid_latent, chosen, slot_ids, scales, router, fc_in, fc_out):
    model_width = mid_tokens.shape[1]
    expert_count = router.shape[1]
    capacity = CAP_FACTOR * mid_tokens.shape[0] // expert_count
    slot_total = expert_count * capacity
    expert_in = layer_norm(mid_tokens, scales).astype(jnp.bfloat16)
    logits = jnp.dot(expert_in, router, preferred_element_type=jnp.float32)
    column = jnp.arange(expert_count, dtype=jnp.int32)
    picked = jnp.sum(
        jnp.where(column[None, :] == chosen[:, None], logits, jnp.zeros_like(logits)), axis=1
    )
    gate_value = jax.nn.sigmoid(picked)
    served = slot_ids < capacity
    position = jnp.where(served, chosen * capacity + slot_ids, slot_total)
    places = jnp.arange(slot_total, dtype=jnp.int32)
    to_slot = (places[:, None] == position[None, :]).astype(jnp.bfloat16)
    buffer = jnp.dot(to_slot, expert_in, preferred_element_type=jnp.float32).astype(jnp.bfloat16)
    results, new_bottleneck = exchange_experts(
        mid_latent.reshape(-1, model_width), buffer, fc_in[0], fc_out[0], expert_count
    )
    from_slot = (position[:, None] == places[None, :]).astype(jnp.bfloat16)
    returned = jnp.dot(from_slot, results, preferred_element_type=jnp.float32)
    mixed = (mid_tokens + gate_value[:, None] * returned).astype(jnp.bfloat16)
    return mixed, new_bottleneck.reshape(mid_latent.shape)


def on_device(
    tokens,
    bottleneck,
    clip_ids,
    expert_ids,
    slots,
    norm1_gain,
    attn_qkv,
    attn_out,
    norm2_gain,
    router,
    fc_in,
    fc_out,
):
    clip_start = lax.axis_index("exp") * bottleneck.shape[0]
    mid_tokens, mid_latent = attend(
        tokens[0], bottleneck, clip_ids[0], clip_start, norm1_gain[0], attn_qkv[0], attn_out[0]
    )
    mixed_tokens, new_bottleneck = mixture(
        mid_tokens, mid_latent, expert_ids[0], slots[0], norm2_gain[0], router, fc_in, fc_out
    )
    return (mixed_tokens[None], new_bottleneck)


def solution(mesh):
    in_specs = (
        P("mod", "exp", None),
        P("exp", None, None),
        P("mod", "exp"),
        P("mod", "exp"),
        P("mod", "exp"),
        P("mod", None),
        P("mod", None, None),
        P("mod", None, None),
        P("mod", None),
        P(),
        P("exp", None, None),
        P("exp", None, None),
    )
    out_specs = (P("mod", "exp", None), P("exp", None, None))
    return jax.shard_map(
        on_device, mesh=mesh, in_specs=in_specs, out_specs=out_specs, check_vma=False
    )
```

profile of v0, /device:TPU:0, one launch (start us, length us, event | category | flops | bytes accessed | tf_op | source)
XLA Modules:
  0.0 135.5 jit_solution(18094258901326215341)
XLA Ops:
  0.6 0.0 copy-start
  0.6 0.0 copy-start.1
  0.7 0.9 add_select_fusion
  1.5 0.8 compare_select_fusion
  2.3 0.7 pad_add_fusion
  3.0 0.7 mul.88
  3.7 0.7 mul.89
  4.4 0.8 reshape.56
  5.2 1.5 %convert_reduce_fusion = f32[528]{0:T(1024)S(1)} fusion(bf16[16,1024]{1,0:T(8,128)(2,1)S(1)} %reshape.56, bf16[512,1024]{1,0:T(8,128)(2,1)} %bitcast.28), kind=kLoop, calls=%fused_computation.5 | loop fusion | flops 2702832 | bytes 1083456 | tf_op jit(solution)/shard_map/reduce_sum | solution.py:20
  6.6 1.7 %fusion.7 = f32[528]{0:T(1024)S(1)} fusion(f32[528]{0:T(1024)S(1)} %broadcast_multiply_fusion, bf16[16,1024]{1,0:T(8,128)(2,1)S(1)} %reshape.56, bf16[512,1024]{1,0:T(8,128)(2,1)} %bitcast.29), kind=kLoop, calls=%fused_computation.8 | loop fusion | flops 3784176 | bytes 1085568 | tf_op jit(solution)/shard_map/reduce_sum | solution.py:22
  8.3 0.1 broadcast_in_dim.36.rows_ref
  8.4 0.0 copy-done.1
  8.4 7.1 %fusion.2.q_ref.k_ref.v_ref = bf16[528,3072]{1,0:T(8,128)(2,1)S(1)} fusion(bf16[1,1024,3072]{2,1,0:T(8,128)(2,1)} %param.18, f32[1024]{0:T(1024)S(1)} %bitcast.36, f32[528]{0:T(1024)S(1)} %add_rsqrt_fusion, f32[528]{0:T(1024)S(1)} %broadcast_multiply_fusion, bf16[16,1024]{1,0:T(8,128)(2,1)S(1)} %reshape.56, bf16[512,1024]{1,0:T(8,128)(2,1)S(1)} %bitcast.30), kind=kOutput, calls=%fused_computation.2 | convolution fusion | flops 3327836160 | bytes 10625152 | tf_op jit(solution)/shard_map/dot_general | solution.py:81
  15.6 14.4 %shard_map.131 = bf16[528,1024]{1,0:T(8,128)(2,1)S(1)} custom-call(s32[528,1]{1,0:T(8,128)S(1)} %broadcast_in_dim.36.rows_ref, s32[1,528]{1,0:T(1,128)S(1)} %broadcast_in_dim.15.cols_ref, bf16[528,3072]{1,0:T(8,128)(2,1)S(1)} %fusion.2.q_ref.k_ref.v_ref, bf16[528,3072]{1,0:T(8,128)(2,1)S(1)} %fusion.2.q_ref.k_ref.v_ref, ...), custom_call_target="tpu_custom_call" | custom-call | tf_op jit(solution)/shard_map/pallas_call | solution.py:57
  30.0 0.0 copy-done
  30.0 1.3 convert_add_fusion
  31.3 0.2 slice_reduce_fusion
  31.5 0.3 multiply_reduce_fusion
  31.9 0.0 copy-start.2
  31.9 0.0 copy-start.3
  31.9 0.3 multiply_convert_fusion
  32.3 0.4 copy-done.2
  32.6 0.0 copy-done.3
  32.6 0.4 fusion.18
  33.1 1.3 fusion.14.buf_ref
  34.3 98.2 %shard_map.132 = (bf16[1024,1024]{1,0:T(8,128)(2,1)S(1)}, bf16[16,1024]{1,0:T(8,128)(2,1)S(1)}) custom-call(f32[16,1024]{1,0:T(8,128)S(1)} %slice.9.latent_ref, bf16[1024,1024]{1,0:T(8,128)(2,1)S(1)} %fusion.14.buf_ref, bf16[1024,4096]{1,0:T(8,128)(2,1)} %bitcast.26, bf16[4096,1024]{1,0:T(8,128)(2,1)} %bitcast.27), custom_call_target="tpu_custom_call" | custom-call | tf_op jit(solution)/shard_map/pallas_call | solution.py:250
  132.6 2.3 %fusion.17 = bf16[1,512,1024]{2,1,0:T(8,128)(2,1)} fusion(bf16[1024,1024]{1,0:T(8,128)(2,1)S(1)} %get-tuple-element.4, f32[528,1024]{1,0:T(8,128)S(1)} %convert_add_fusion, s32[512]{0:T(512)S(1)} %add_select_fusion, f32[512]{0:T(512)S(1)} %add_divide_fusion), kind=kOutput, calls=%fused_computation.22 | convolution fusion | flops 1075838976 | bytes 5246976 | tf_op jit(solution)/shard_map/dot_general | solution.py:301
  134.8 0.6 reshape.57
  (8 shorter events, 0.0 us)
Async XLA Ops:
  0.6 29.4 %copy-start = (bf16[1,1024,1024]{2,1,0:T(8,128)(2,1)S(1)}, bf16[1,1024,1024]{2,1,0:T(8,128)(2,1)}, u32[]{:S(2)}) copy-start(bf16[1,1024,1024]{2,1,0:T(8,128)(2,1)} %param.19) | copy-start | bytes 6291460
  0.6 7.8 %copy-start.1 = (bf16[1,512,1024]{2,1,0:T(8,128)(2,1)S(1)}, bf16[1,512,1024]{2,1,0:T(8,128)(2,1)}, u32[]{:S(2)}) copy-start(bf16[1,512,1024]{2,1,0:T(8,128)(2,1)} %param.12) | copy-start | bytes 3145732
  31.9 0.8 copy-start.2
  31.9 0.8 copy-start.3
where the time goes:
time: 136 us; the launch traced here: 135 us
  Pallas kernels  113 us (83%)
  matrix products  12.4 us (9%)
  other arithmetic  7.71 us (6%)
  local copies, waits for them, and re-layouts  1.95 us (1%)
    pallas_call x1, Pallas kernels, exchange_experts(): pl.pallas_call(functools.partial(moe_kernel, size, cap, tile), out_shape=...  98.2 us
    pallas_call x1, Pallas kernels, attention(): pl.pallas_call(functools.partial(attention_kernel, pair), grid=(steps,),...  14.4 us
    dot_general x1, matrix products, attend(): jnp.dot(normed, w_qkv, preferred_element_type=jnp.float32)  7.12 us

commit v1 on v0

v1 whole, which is shorter than its diff:
```python
import functools
import math

import jax
import jax.numpy as jnp
from jax import lax
from jax.experimental import pallas as pl
from jax.experimental.pallas import tpu as pltpu
from jax.sharding import PartitionSpec as P

MESH = pl.DeviceIdType.MESH
HEAD = 64
CAP_FACTOR = 2
EARLY = 128
PAIRS = 2
NEAR = 4


EPSILON = 1e-06


def layer_norm(features, scales):
    row_mean = jnp.mean(features, axis=-1, keepdims=True)
    centred = features - row_mean
    spread = jnp.mean(centred * centred, axis=-1, keepdims=True)
    return centred * lax.rsqrt(spread + EPSILON) * scales


def gelu(x):
    half = 0.5 * x
    return half + half * lax.erf(x * (1.0 / math.sqrt(2.0)))


def matmul(lhs, rhs):
    return jnp.dot(lhs, rhs, preferred_element_type=jnp.float32)


def one_hot(condition):
    return jnp.where(condition, 1.0, 0.0).astype(jnp.bfloat16)


def to_column(row):
    return jnp.transpose(jnp.broadcast_to(row, (128, row.shape[1])))


def layer_kernel(
    size,
    cap,
    tile,
    tok_hbm,
    latent_ref,
    clip_ref,
    expert_ref,
    slot_ref,
    gain1_ref,
    gain2_ref,
    router_ref,
    qkv_hbm,
    proj_hbm,
    w_in_hbm,
    w_out_hbm,
    out_ref,
    mean_ref,
    rows_ref,
    normed,
    w_qkv,
    w_proj,
    w_in,
    w_out,
    kv,
    queries,
    attended,
    bias,
    mid,
    expert_in,
    gates,
    places,
    sorted_place,
    buf,
    recv,
    res,
    back,
    acc,
    act,
    my_latent,
    peer_latent,
    tok_sem,
    qkv_sems,
    w_sems,
    lat_sems,
    send_sems,
    recv_sems,
    back_send,
    back_recv,
):
    near = NEAR if size % NEAR == 0 else 1
    far = size // near
    me = lax.axis_index("exp")
    mod = lax.axis_index("mod")
    high, low = me // near, me % near
    shifts = [0] + sorted(range(1, far), key=lambda s: (abs(2 * s - far), s))
    order = [(s, d) for s in shifts for d in range(near)]

    def ahead(step):
        s, d = order[step]
        return ((high + s) % far) * near + (low + d) % near

    def behind(step):
        s, d = order[step]
        return ((high + far - s) % far) * near + (low + near - d) % near

    def slots_of(step):
        return pl.ds(step * cap, cap)

    tokens = tok_hbm.shape[0]
    clips, per_clip, width = latent_ref.shape
    latents = clips * per_clip
    row_count = tokens + latents
    key_count = kv.shape[0]
    slot_total = size * cap

    load_tok = pltpu.make_async_copy(tok_hbm, rows_ref.at[pl.ds(0, tokens)], tok_sem)
    load_tok.start()
    loads = []
    for index in (1, 2, 0):
        cols = pl.ds(index * width, width)
        loads.append(
            pltpu.make_async_copy(qkv_hbm.at[:, cols], w_qkv.at[:, cols], qkv_sems.at[index])
        )
        loads[-1].start()
    load_k, load_v, load_q = loads
    load_proj = pltpu.make_async_copy(proj_hbm, w_proj, w_sems.at[2])
    load_in = pltpu.make_async_copy(w_in_hbm, w_in, w_sems.at[0])
    load_out = pltpu.make_async_copy(w_out_hbm, w_out, w_sems.at[1])
    load_proj.start()

    barrier = pltpu.get_barrier_semaphore()
    for step in range(1, size):
        pl.semaphore_signal(barrier, inc=1, device_id=(mod, ahead(step)), device_id_type=MESH)
    pl.semaphore_signal(barrier, inc=1, device_id=(1 - mod, me), device_id_type=MESH)

    sends = [None]
    backs = [None]
    for step in range(1, size):
        sends.append(
            pltpu.make_async_remote_copy(
                src_ref=buf.at[slots_of(step)],
                dst_ref=recv.at[slots_of(step)],
                send_sem=send_sems.at[step],
                recv_sem=recv_sems.at[step],
                device_id=(mod, ahead(step)),
                device_id_type=MESH,
            )
        )
        backs.append(
            pltpu.make_async_remote_copy(
                src_ref=res.at[slots_of(step)],
                dst_ref=back.at[slots_of(step)],
                send_sem=back_send.at[step],
                recv_sem=back_recv.at[step],
                device_id=(mod, behind(step)),
                device_id_type=MESH,
            )
        )

    experts = expert_ref[...]
    slots = slot_ref[...]
    served = slots < cap
    walk = list(range(near, size)) + list(range(near))
    steps = jnp.zeros_like(experts)
    rank = jnp.zeros_like(experts)
    start = jnp.zeros((1, 1), jnp.int32)
    lost = jnp.zeros((1, 1), jnp.int32)
    lost_rank = jnp.zeros_like(experts)
    for step in walk:
        here = experts == ahead(step)
        steps = jnp.where(here, step, steps)
        rank = jnp.where(here, start + slots, rank)
        lost_rank = jnp.where(here, lost + slots - cap, lost_rank)
        count = jnp.sum(jnp.where(here, 1.0, 0.0), axis=1, keepdims=True).astype(jnp.int32)
        start = start + jnp.minimum(count, cap)
        lost = lost + jnp.maximum(count - cap, 0)
    rank = jnp.where(served, rank, start + lost_rank)
    place_row = jnp.where(served, steps * cap + slots, slot_total)

    lane = lax.broadcasted_iota(jnp.int32, (1, key_count - tokens), 1)
    latent_clip = jnp.where(lane < latents, lane // per_clip, -1)
    token_clip = clip_ref[...] - me * clips
    clip_row = jnp.concatenate([token_clip, latent_clip], axis=1).astype(jnp.float32)

    field = lax.broadcasted_iota(jnp.int32, (16, tokens), 0)
    facts = jnp.where(
        field == 0,
        jnp.where(served, steps, size),
        jnp.where(field == 1, jnp.where(served, slots, 0), 0),
    ).astype(jnp.float32).astype(jnp.bfloat16)

    gain1 = gain1_ref[...].astype(jnp.float32)
    gain2 = gain2_ref[...].astype(jnp.float32)
    kv[pl.ds(row_count, key_count - row_count), :] = jnp.zeros(
        (key_count - row_count, kv.shape[1]), jnp.bfloat16
    )
    rows_ref[pl.ds(tokens, latents), :] = jnp.concatenate(
        [latent_ref[clip].astype(jnp.float32) for clip in range(clips)], axis=0
    ).astype(jnp.bfloat16)
    load_tok.wait()
    chunk = 48

    def norm1(i, carry):
        here = pl.ds(pl.multiple_of(i * chunk, 16), chunk)
        normed[here, :] = layer_norm(rows_ref[here, :].astype(jnp.float32), gain1).astype(
            jnp.bfloat16
        )
        return carry

    lax.fori_loop(0, row_count // chunk, norm1, 0)

    step_cols = 256

    def project_kv(load, offset):
        load.wait()

        def body(i, carry):
            src = pl.ds(pl.multiple_of(width + offset + i * step_cols, 128), step_cols)
            dst = pl.ds(pl.multiple_of(offset + i * step_cols, 128), step_cols)
            kv[pl.ds(0, row_count), dst] = matmul(normed[...], w_qkv[:, src]).astype(jnp.bfloat16)
            return carry

        lax.fori_loop(0, width // step_cols, body, 0)

    project_kv(load_k, 0)
    project_kv(load_v, width)

    pair = 128 // HEAD

    def attend(here, rows):
        def body(i, carry):
            for sub in range(PAIRS):
                p = i * PAIRS + sub
                cols = pl.ds(pl.multiple_of(p * 128, 128), 128)
                v_cols = pl.ds(pl.multiple_of(width + p * 128, 128), 128)
                key_block = kv[:, cols]
                value_block = kv[:, v_cols]
                query_block = queries[here, cols]
                head_of = lax.broadcasted_iota(jnp.int32, query_block.shape, 1) // HEAD
                total = jnp.zeros(query_block.shape, jnp.float32)
                for head in range(pair):
                    mine = head_of == head
                    scores = lax.dot_general(
                        jnp.where(mine, query_block, jnp.zeros_like(query_block)),
                        key_block,
                        (((1,), (1,)), ((), ())),
                        preferred_element_type=jnp.float32,
                    )
                    scores = scores + bias[here, :]
                    weights = jnp.exp(scores - jnp.max(scores, axis=-1, keepdims=True))
                    norm = jnp.sum(weights, axis=-1, keepdims=True)
                    summed = matmul(weights.astype(jnp.bfloat16), value_block)
                    total = jnp.where(mine, summed / norm, total)
                attended[here, cols] = total.astype(jnp.bfloat16)
            return carry

        lax.fori_loop(0, width // 128 // PAIRS, body, 0)

    inverse_root = jnp.bfloat16(1.0 / math.sqrt(HEAD))

    def project_q(first, rows):
        here = pl.ds(first, rows)

        def body(i, carry):
            cols = pl.ds(pl.multiple_of(i * step_cols, 128), step_cols)
            queries[here, cols] = (
                matmul(attended[here, :], w_qkv[:, cols]).astype(jnp.bfloat16) * inverse_root
            )
            return carry

        lax.fori_loop(0, width // step_cols, body, 0)

    row_in = lax.broadcasted_iota(jnp.int32, (EARLY, 1), 0)

    def gather(piece):
        here = pl.ds(piece * EARLY, EARLY)
        chosen = (piece * EARLY + row_in) == rank
        pick = one_hot(chosen)
        clip = jnp.sum(jnp.where(chosen, clip_row[:, :tokens], 0.0), axis=1, keepdims=True)
        bias[here, :] = jnp.where(clip == clip_row, 0.0, -jnp.inf)
        moved = lax.dot_general(
            facts, pick, (((1,), (1,)), ((), ())), preferred_element_type=jnp.float32
        ).astype(jnp.int32)
        at = moved[0:1, :] * cap + moved[1:2, :]
        sorted_place[:, here] = at
        attended[here, :] = matmul(pick, normed[pl.ds(0, tokens), :]).astype(jnp.bfloat16)
        acc[here, :] = matmul(pick, rows_ref[pl.ds(0, tokens), :])

    slot_row = lax.broadcasted_iota(jnp.int32, (128, 1), 0)

    def finish(piece):
        here = pl.ds(piece * EARLY, EARLY)
        attend(here, EARLY)
        if piece == 0:
            load_proj.wait()

        def project_out(i, carry):
            cols = pl.ds(pl.multiple_of(i * step_cols, 128), step_cols)
            acc[here, cols] += matmul(attended[here, :], w_proj[:, cols])
            return carry

        lax.fori_loop(0, width // step_cols, project_out, 0)
        half = EARLY // 2
        for part in range(2):
            some = pl.ds(piece * EARLY + part * half, half)
            expert_in[some, :] = layer_norm(acc[some, :], gain2).astype(jnp.bfloat16)

    def dispatch(base, count, known):
        pick = one_hot((base + slot_row[:count]) == sorted_place[:, pl.ds(0, known)])
        buf[pl.ds(base, count), :] = matmul(pick, expert_in[pl.ds(0, known), :]).astype(
            jnp.bfloat16
        )
        for step in range(base // cap, (base + count) // cap):
            if step:
                sends[step].start()
            else:
                recv[slots_of(0), :] = buf[slots_of(0), :]

    pieces = tokens // EARLY
    load_q.wait()
    gather(0)
    project_q(0, EARLY)
    finish(0)
    pl.semaphore_wait(barrier, size)
    base = near * cap
    dispatch(base, 128, EARLY)
    load_in.start()
    load_out.start()
    for piece in range(1, pieces):
        gather(piece)
    attended[pl.ds(tokens, latents), :] = normed[pl.ds(tokens, latents), :]
    project_q(EARLY, row_count - EARLY)
    for piece in range(1, pieces - 1):
        finish(piece)
        base += 128
        dispatch(base, 128, (piece + 1) * EARLY)
    finish(pieces - 1)
    for base in list(range(base + 128, slot_total, 128)) + list(range(0, near * cap, 128)):
        count = min(128, slot_total - base, near * cap - base if base < near * cap else 128)
        dispatch(base, count, tokens)

    tail = pl.ds(tokens, latents)
    tail_clip = lax.broadcasted_iota(jnp.int32, (latents, 1), 0) // per_clip
    bias[tail, :] = jnp.where(tail_clip.astype(jnp.float32) == clip_row, 0.0, -jnp.inf)
    attend(tail, latents)
    my_latent[...] = rows_ref[tail, :].astype(jnp.float32) + matmul(attended[tail, :], w_proj[...])
    latent_copy = pltpu.make_async_remote_copy(
        src_ref=my_latent,
        dst_ref=peer_latent,
        send_sem=lat_sems.at[0],
        recv_sem=lat_sems.at[1],
        device_id=(1 - mod, me),
        device_id_type=MESH,
    )
    latent_copy.start()

    logits = lax.dot_general(
        expert_in[...],
        router_ref[...],
        (((1,), (1,)), ((), ())),
        preferred_element_type=jnp.float32,
    )
    rank_col = to_column(rank.astype(jnp.float32)).astype(jnp.int32)
    places[...] = to_column(place_row.astype(jnp.float32)).astype(jnp.int32)
    expert_col = to_column(experts.astype(jnp.float32)).astype(jnp.int32)
    column = lax.broadcasted_iota(jnp.int32, (EARLY, size), 1)
    sorted_row = lax.broadcasted_iota(jnp.int32, (1, tokens), 1)

    def split(value):
        top = value.astype(jnp.bfloat16)
        return top, value - top.astype(jnp.float32)

    high_logits, rest = split(logits)
    middle_logits, rest = split(rest)
    low_logits, _ = split(rest)
    for piece in range(pieces):
        here = pl.ds(piece * EARLY, EARLY)
        pick = one_hot(rank_col[piece * EARLY : (piece + 1) * EARLY, 0:1] == sorted_row)
        own = (matmul(pick, high_logits) + matmul(pick, middle_logits)) + matmul(pick, low_logits)
        mine = column == expert_col[piece * EARLY : (piece + 1) * EARLY, 0:1]
        picked = jnp.sum(jnp.where(mine, own, 0.0), axis=1, keepdims=True)
        gates[here, :] = jnp.broadcast_to(jax.nn.sigmoid(picked), (EARLY, 128))

        def restore(i, carry):
            cols = pl.ds(pl.multiple_of(i * step_cols, 128), step_cols)
            first, rest = split(acc[:, cols])
            second, rest = split(rest)
            third, _ = split(rest)
            mid[here, cols] = (matmul(pick, first) + matmul(pick, second)) + matmul(pick, third)
            return carry

        lax.fori_loop(0, width // step_cols, restore, 0)

    groups = 2 if size % 4 == 0 else 1
    steps_per = size // groups
    group_rows = steps_per * cap
    tiles = w_in.shape[1] // tile
    for g in range(groups):
        for step in range(g * steps_per, (g + 1) * steps_per):
            if step:
                sends[step].wait_recv()
        if g == 0:
            load_in.wait()
            load_out.wait()
        here = pl.ds(g * group_rows, group_rows)

        def hidden(t):
            cols = pl.ds(pl.multiple_of(t * tile, tile), tile)
            return gelu(matmul(recv[here, :], w_in[:, cols])).astype(jnp.bfloat16)

        def project(t, slot):
            cols = pl.ds(pl.multiple_of(t * tile, tile), tile)
            return matmul(act[slot], w_out[cols, :])

        act[0] = hidden(0)
        acc[...] = jnp.zeros_like(acc)

        def body(t, carry):
            acc[...] += project(t - 1, (t + 1) % 2)
            act[t % 2] = hidden(t)
            return carry

        lax.fori_loop(1, tiles, body, 0)
        res[here, :] = (acc[...] + project(tiles - 1, (tiles - 1) % 2)).astype(jnp.bfloat16)
        for step in range(g * steps_per, (g + 1) * steps_per):
            if step:
                backs[step].start()
            else:
                back[slots_of(0), :] = res[slots_of(0), :]

    latent_copy.wait()
    mean = (my_latent[...] + peer_latent[...]) * 0.5
    for clip in range(clips):
        mean_ref[clip] = mean[clip * per_clip : (clip + 1) * per_clip, :].astype(jnp.bfloat16)

    for g in range(groups):
        for step in range(g * steps_per, (g + 1) * steps_per):
            if step:
                backs[step].wait_recv()

        def combine(i, carry):
            here = pl.ds(pl.multiple_of(i * 128, 128), 128)
            slot = lax.broadcasted_iota(jnp.int32, (1, group_rows), 1) + g * group_rows
            pick = one_hot(places[here, 0:1] == slot)
            returned = matmul(pick, back[pl.ds(g * group_rows, group_rows), :])
            mixed = mid[here, :] + gates[here, 0:1] * returned
            if g == groups - 1:
                out_ref[here, :] = mixed.astype(jnp.bfloat16)
            else:
                mid[here, :] = mixed
            return carry

        lax.fori_loop(0, tokens // 128, combine, 0)
    for step in range(1, size):
        sends[step].wait_send()
        backs[step].wait_send()


def layer(
    tokens, bottleneck, clip, expert, slot, gain1, gain2, router, w_qkv, w_proj, w_in, w_out, size
):
    count, width = tokens.shape
    latents = bottleneck.shape[0] * bottleneck.shape[1]
    hidden_width = w_in.shape[1]
    rows = count + latents
    keys = count + 128
    cap = CAP_FACTOR * count // size
    slots = size * cap
    groups = 2 if size % 4 == 0 else 1
    tile = 1024
    vmem = pl.BlockSpec(memory_space=pltpu.VMEM)
    hbm = pl.BlockSpec(memory_space=pl.ANY)
    bf16, f32 = jnp.bfloat16, jnp.float32
    dma = pltpu.SemaphoreType.DMA
    return pl.pallas_call(
        functools.partial(layer_kernel, size, cap, tile),
        out_shape=(
            jax.ShapeDtypeStruct((count, width), bf16),
            jax.ShapeDtypeStruct(bottleneck.shape, bf16),
        ),
        in_specs=[hbm] + [vmem] * 7 + [hbm] * 4,
        out_specs=(vmem, vmem),
        scratch_shapes=[
            pltpu.VMEM((rows, width), bf16),
            pltpu.VMEM((rows, width), bf16),
            pltpu.VMEM((width, 3 * width), bf16),
            pltpu.VMEM((width, width), bf16),
            pltpu.VMEM((width, hidden_width), bf16),
            pltpu.VMEM((hidden_width, width), bf16),
            pltpu.VMEM((keys, 2 * width), bf16),
            pltpu.VMEM((rows, width), bf16),
            pltpu.VMEM((rows, width), bf16),
            pltpu.VMEM((rows, keys), f32),
            pltpu.VMEM((count, width), f32),
            pltpu.VMEM((count, width), bf16),
            pltpu.VMEM((count, 128), f32),
            pltpu.VMEM((count, 128), jnp.int32),
            pltpu.VMEM((1, count), jnp.int32),
            pltpu.VMEM((slots, width), bf16),
            pltpu.VMEM((slots, width), bf16),
            pltpu.VMEM((slots, width), bf16),
            pltpu.VMEM((slots, width), bf16),
            pltpu.VMEM((slots // groups, width), f32),
            pltpu.VMEM((2, slots // groups, tile), bf16),
            pltpu.VMEM((latents, width), f32),
            pltpu.VMEM((latents, width), f32),
            dma(()),
            dma((3,)),
            dma((3,)),
            dma((2,)),
            dma((size,)),
            dma((size,)),
            dma((size,)),
            dma((size,)),
        ],
        compiler_params=pltpu.CompilerParams(
            collective_id=0, has_side_effects=True, vmem_limit_bytes=56 * 1024 * 1024
        ),
    )(tokens, bottleneck, clip, expert, slot, gain1, gain2, router, w_qkv, w_proj, w_in, w_out)


def on_device(
    size,
    tokens,
    bottleneck,
    clip_ids,
    expert_ids,
    slots,
    norm1_gain,
    attn_qkv,
    attn_out,
    norm2_gain,
    router,
    fc_in,
    fc_out,
):
    mixed, latent = layer(
        tokens[0],
        bottleneck,
        clip_ids,
        expert_ids,
        slots,
        norm1_gain,
        norm2_gain,
        router.T,
        attn_qkv[0],
        attn_out[0],
        fc_in[0],
        fc_out[0],
        size,
    )
    return (mixed[None], latent)


def solution(mesh):
    in_specs = (
        P("mod", "exp", None),
        P("exp", None, None),
        P("mod", "exp"),
        P("mod", "exp"),
        P("mod", "exp"),
        P("mod", None),
        P("mod", None, None),
        P("mod", None, None),
        P("mod", None),
        P(),
        P("exp", None, None),
        P("exp", None, None),
    )
    out_specs = (P("mod", "exp", None), P("exp", None, None))
    return jax.shard_map(
        functools.partial(on_device, mesh.shape["exp"]),
        mesh=mesh,
        in_specs=in_specs,
        out_specs=out_specs,
        check_vma=False,
    )
```

time: 136 us -> 121 us (0.89)
  the two profiles are of different devices: /device:TPU:0 before, /device:TPU:9 now
where the time goes in v1:
time: 121 us
  Pallas kernels  117 us (97%)
  local copies, waits for them, and re-layouts  3.65 us (3%)
    pallas_call x1, Pallas kernels, layer(): pl.pallas_call(functools.partial(layer_kernel, size, cap, tile), out_shap...  117 us
    unnamed x2, local copies, waits for them, and re-layouts  3.65 us

profile of v1, /device:TPU:9, one launch (start us, length us, event | category | flops | bytes accessed | tf_op | source)
XLA Modules:
  0.0 120.9 jit_solution(6576941600569476249)
XLA Ops:
  0.6 116.6 %shard_map.131 = (bf16[512,1024]{1,0:T(8,128)(2,1)}, bf16[4,4,1024]{2,1,0:T(4,128)(2,1)}) custom-call(bf16[512,1024]{1,0:T(8,128)(2,1)} %bitcast.12, bf16[4,4,1024]{2,1,0:T(4,128)(2,1)} %latent_ref.1, s32[1,512]{1,0:T(1,128)} %clip_ref.1, s32[1,512]{1,0:T(1,128)} %expert_ref.1, s32[1,512]{1,0:T(1,128)} %slot_ref.1, bf16[1,1024]{1,0:T(2,128)(2,1)} %gain1_ref.1, ...), custom_call_target="tpu_custom_call" | custom-call | tf_op jit(solution)/shard_map/pallas_call | solution.py:481
  117.3 2.3 %copy.16 = bf16[1,512,1024]{2,1,0:T(8,128)(2,1)} copy(bf16[1,512,1024]{2,1,0:T(8,128)(2,1)} %bitcast.11) | data formatting | bytes 2097152
  119.5 1.4 %copy.17 = bf16[4,4,1024]{2,1,0:T(4,128)(2,1)} copy(bf16[4,4,1024]{2,1,0:T(4,128)(2,1)} %get-tuple-element.9) | data formatting | bytes 65536

commit v2 on v1

--- a/solution.py
+++ b/solution.py
@@ -12,6 +12,7 @@
 HEAD = 64
 CAP_FACTOR = 2
 EARLY = 128
+FEW = 64
 PAIRS = 2
 NEAR = 4
 
@@ -48,6 +49,19 @@
     cap,
     tile,
     tok_hbm,
+    latent_hbm,
+    clip_hbm,
+    expert_hbm,
+    slot_hbm,
+    gain1_hbm,
+    gain2_hbm,
+    router_hbm,
+    qkv_hbm,
+    proj_hbm,
+    w_in_hbm,
+    w_out_hbm,
+    out_ref,
+    mean_ref,
     latent_ref,
     clip_ref,
     expert_ref,
@@ -55,19 +69,15 @@
     gain1_ref,
     gain2_ref,
     router_ref,
-    qkv_hbm,
-    proj_hbm,
-    w_in_hbm,
-    w_out_hbm,
-    out_ref,
-    mean_ref,
     rows_ref,
     normed,
     w_qkv,
     w_proj,
     w_in,
     w_out,
-    kv,
+    key_ref,
+    value_t,
+    key_clips,
     queries,
     attended,
     bias,
@@ -76,15 +86,18 @@
     gates,
     places,
     sorted_place,
+    row_clips,
     buf,
     recv,
     res,
     back,
     acc,
     act,
+    sums,
     my_latent,
     peer_latent,
     tok_sem,
+    small_sems,
     qkv_sems,
     w_sems,
     lat_sems,
@@ -116,23 +129,38 @@
     clips, per_clip, width = latent_ref.shape
     latents = clips * per_clip
     row_count = tokens + latents
-    key_count = kv.shape[0]
+    key_count = key_ref.shape[0]
     slot_total = size * cap
 
     load_tok = pltpu.make_async_copy(tok_hbm, rows_ref.at[pl.ds(0, tokens)], tok_sem)
     load_tok.start()
+    small = [
+        pltpu.make_async_copy(src, dst, small_sems.at[index])
+        for index, (src, dst) in enumerate(
+            (
+                (expert_hbm, expert_ref),
+                (slot_hbm, slot_ref),
+                (clip_hbm, clip_ref),
+                (gain1_hbm, gain1_ref),
+                (latent_hbm, latent_ref),
+                (gain2_hbm, gain2_ref),
+                (router_hbm, router_ref),
+            )
+        )
+    ]
+    for copy in small:
+        copy.start()
     loads = []
     for index in (1, 2, 0):
         cols = pl.ds(index * width, width)
         loads.append(
             pltpu.make_async_copy(qkv_hbm.at[:, cols], w_qkv.at[:, cols], qkv_sems.at[index])
         )
-        loads[-1].start()
     load_k, load_v, load_q = loads
+    load_k.start()
     load_proj = pltpu.make_async_copy(proj_hbm, w_proj, w_sems.at[2])
     load_in = pltpu.make_async_copy(w_in_hbm, w_in, w_sems.at[0])
     load_out = pltpu.make_async_copy(w_out_hbm, w_out, w_sems.at[1])
-    load_proj.start()
 
     barrier = pltpu.get_barrier_semaphore()
     for step in range(1, size):
@@ -163,6 +191,8 @@
             )
         )
 
+    for copy in small:
+        copy.wait()
     experts = expert_ref[...]
     slots = slot_ref[...]
     served = slots < cap
@@ -192,18 +222,23 @@
     facts = jnp.where(
         field == 0,
         jnp.where(served, steps, size),
-        jnp.where(field == 1, jnp.where(served, slots, 0), 0),
+        jnp.where(
+            field == 1, jnp.where(served, slots, 0), jnp.where(field == 2, token_clip, 0)
+        ),
     ).astype(jnp.float32).astype(jnp.bfloat16)
 
     gain1 = gain1_ref[...].astype(jnp.float32)
     gain2 = gain2_ref[...].astype(jnp.float32)
-    kv[pl.ds(row_count, key_count - row_count), :] = jnp.zeros(
-        (key_count - row_count, kv.shape[1]), jnp.bfloat16
-    )
+    key_clips[...] = to_column(clip_row)
+    padding = key_count - row_count
+    key_ref[pl.ds(row_count, padding), :] = jnp.zeros((padding, width), jnp.bfloat16)
     rows_ref[pl.ds(tokens, latents), :] = jnp.concatenate(
         [latent_ref[clip].astype(jnp.float32) for clip in range(clips)], axis=0
     ).astype(jnp.bfloat16)
     load_tok.wait()
+    load_v.start()
+    load_q.start()
+    load_proj.start()
     chunk = 48
 
     def norm1(i, carry):
@@ -217,47 +252,95 @@
 
     step_cols = 256
 
-    def project_kv(load, offset):
-        load.wait()
-
-        def body(i, carry):
-            src = pl.ds(pl.multiple_of(width + offset + i * step_cols, 128), step_cols)
-            dst = pl.ds(pl.multiple_of(offset + i * step_cols, 128), step_cols)
-            kv[pl.ds(0, row_count), dst] = matmul(normed[...], w_qkv[:, src]).astype(jnp.bfloat16)
-            return carry
-
-        lax.fori_loop(0, width // step_cols, body, 0)
-
-    project_kv(load_k, 0)
-    project_kv(load_v, width)
+    def project_key(i, carry):
+        src = pl.ds(pl.multiple_of(width + i * step_cols, 128), step_cols)
+        dst = pl.ds(pl.multiple_of(i * step_cols, 128), step_cols)
+        key_ref[pl.ds(0, row_count), dst] = matmul(normed[...], w_qkv[:, src]).astype(jnp.bfloat16)
+        return carry
+
+    def project_value(i, carry):
+        src = pl.ds(pl.multiple_of(2 * width + i * step_cols, 128), step_cols)
+        dst = pl.ds(pl.multiple_of(i * step_cols, 128), step_cols)
+        block = matmul(normed[...], w_qkv[:, src]).astype(jnp.bfloat16)
+        zeros = jnp.zeros((padding, step_cols), jnp.bfloat16)
+        value_t[dst, :] = jnp.transpose(jnp.concatenate([block, zeros], axis=0))
+        return carry
+
+    load_k.wait()
+    lax.fori_loop(0, width // step_cols, project_key, 0)
+    load_v.wait()
+    lax.fori_loop(0, width // step_cols, project_value, 0)
 
     pair = 128 // HEAD
 
-    def attend(here, rows):
+    def attend_few(first):
+        here = pl.ds(first, FEW)
+        wide = 2 * 128
+
         def body(i, carry):
             for sub in range(PAIRS):
-                p = i * PAIRS + sub
-                cols = pl.ds(pl.multiple_of(p * 128, 128), 128)
-                v_cols = pl.ds(pl.multiple_of(width + p * 128, 128), 128)
-                key_block = kv[:, cols]
-                value_block = kv[:, v_cols]
-                query_block = queries[here, cols]
-                head_of = lax.broadcasted_iota(jnp.int32, query_block.shape, 1) // HEAD
-                total = jnp.zeros(query_block.shape, jnp.float32)
-                for head in range(pair):
-                    mine = head_of == head
-                    scores = lax.dot_general(
-                        jnp.where(mine, query_block, jnp.zeros_like(query_block)),
-                        key_block,
-                        (((1,), (1,)), ((), ())),
-                        preferred_element_type=jnp.float32,
-                    )
-                    scores = scores + bias[here, :]
-                    weights = jnp.exp(scores - jnp.max(scores, axis=-1, keepdims=True))
-                    norm = jnp.sum(weights, axis=-1, keepdims=True)
-                    summed = matmul(weights.astype(jnp.bfloat16), value_block)
-                    total = jnp.where(mine, summed / norm, total)
-                attended[here, cols] = total.astype(jnp.bfloat16)
+                at = (i * PAIRS + sub) * wide
+                cols = pl.ds(pl.multiple_of(at, 128), wide)
+                block = queries[here, cols]
+                head_of = lax.broadcasted_iota(jnp.int32, block.shape, 1) // HEAD
+                stacked = jnp.concatenate(
+                    [
+                        jnp.where(head_of == head, block, jnp.zeros_like(block))
+                        for head in range(wide // HEAD)
+                    ],
+                    axis=0,
+                )
+                scores = lax.dot_general(
+                    key_ref[:, cols],
+                    stacked,
+                    (((1,), (1,)), ((), ())),
+                    preferred_element_type=jnp.float32,
+                )
+                scores = scores + jnp.concatenate([bias[...]] * 2, axis=1)
+                weights = jnp.exp(scores - jnp.max(scores, axis=0, keepdims=True))
+                norm = jnp.sum(weights, axis=0, keepdims=True)
+                summed = matmul(value_t[cols, :], weights.astype(jnp.bfloat16))
+                lane_of = lax.broadcasted_iota(jnp.int32, (FEW, 128), 1)
+                for j in range(2):
+                    part = slice(j * 128, (j + 1) * 128)
+                    turned = jnp.transpose(summed[part, part] / norm[:, part])
+                    both = jnp.where(lane_of < HEAD, turned[:FEW], turned[FEW:])
+                    dst = pl.ds(pl.multiple_of(at + j * 128, 128), 128)
+                    attended[here, dst] = both.astype(jnp.bfloat16)
+            return carry
+
+        lax.fori_loop(0, width // wide // PAIRS, body, 0)
+
+    def attend(first):
+        here = pl.ds(first, EARLY)
+
+        def body(i, carry):
+            for sub in range(PAIRS):
+                cols = pl.ds(pl.multiple_of((i * PAIRS + sub) * 128, 128), 128)
+                block = queries[here, cols]
+                head_of = lax.broadcasted_iota(jnp.int32, block.shape, 1) // HEAD
+                stacked = jnp.concatenate(
+                    [jnp.where(head_of == head, block, jnp.zeros_like(block)) for head in range(pair)],
+                    axis=0,
+                )
+                scores = lax.dot_general(
+                    key_ref[:, cols],
+                    stacked,
+                    (((1,), (1,)), ((), ())),
+                    preferred_element_type=jnp.float32,
+                )
+                scores = scores + jnp.concatenate([bias[...]] * pair, axis=1)
+                weights = jnp.exp(scores - jnp.max(scores, axis=0, keepdims=True))
+                norm = jnp.sum(weights, axis=0, keepdims=True)
+                summed = matmul(value_t[cols, :], weights.astype(jnp.bfloat16))
+                heads = [
+                    summed[head * HEAD : (head + 1) * HEAD, head * EARLY : (head + 1) * EARLY]
+                    / norm[:, head * EARLY : (head + 1) * EARLY]
+                    for head in range(pair)
+                ]
+                attended[here, cols] = jnp.transpose(jnp.concatenate(heads, axis=0)).astype(
+                    jnp.bfloat16
+                )
             return carry
 
         lax.fori_loop(0, width // 128 // PAIRS, body, 0)
@@ -278,38 +361,46 @@
 
     row_in = lax.broadcasted_iota(jnp.int32, (EARLY, 1), 0)
 
-    def gather(piece):
-        here = pl.ds(piece * EARLY, EARLY)
-        chosen = (piece * EARLY + row_in) == rank
+    def gather(first, rows):
+        here = pl.ds(first, rows)
+        chosen = (first + row_in[:rows]) == rank
         pick = one_hot(chosen)
-        clip = jnp.sum(jnp.where(chosen, clip_row[:, :tokens], 0.0), axis=1, keepdims=True)
-        bias[here, :] = jnp.where(clip == clip_row, 0.0, -jnp.inf)
         moved = lax.dot_general(
             facts, pick, (((1,), (1,)), ((), ())), preferred_element_type=jnp.float32
-        ).astype(jnp.int32)
+        )
+        row_clips[:, here] = moved[2:3, :]
+        moved = moved.astype(jnp.int32)
         at = moved[0:1, :] * cap + moved[1:2, :]
         sorted_place[:, here] = at
         attended[here, :] = matmul(pick, normed[pl.ds(0, tokens), :]).astype(jnp.bfloat16)
-        acc[here, :] = matmul(pick, rows_ref[pl.ds(0, tokens), :])
+        sums[here, :] = matmul(pick, rows_ref[pl.ds(0, tokens), :])
 
     slot_row = lax.broadcasted_iota(jnp.int32, (128, 1), 0)
 
-    def finish(piece):
-        here = pl.ds(piece * EARLY, EARLY)
-        attend(here, EARLY)
-        if piece == 0:
+    def mask(clips_across):
+        bias[...] = jnp.where(key_clips[...] == clips_across, 0.0, -jnp.inf)
+
+    def finish(first, rows):
+        here = pl.ds(first, rows)
+        if rows == FEW:
+            mask(jnp.concatenate([row_clips[:, here]] * 2, axis=1))
+            attend_few(first)
+        else:
+            mask(row_clips[:, here])
+            attend(first)
+        if first == 0:
             load_proj.wait()
 
         def project_out(i, carry):
             cols = pl.ds(pl.multiple_of(i * step_cols, 128), step_cols)
-            acc[here, cols] += matmul(attended[here, :], w_proj[:, cols])
+            sums[here, cols] += matmul(attended[here, :], w_proj[:, cols])
             return carry
 
         lax.fori_loop(0, width // step_cols, project_out, 0)
-        half = EARLY // 2
+        half = rows // 2
         for part in range(2):
-            some = pl.ds(piece * EARLY + part * half, half)
-            expert_in[some, :] = layer_norm(acc[some, :], gain2).astype(jnp.bfloat16)
+            some = pl.ds(first + part * half, half)
+            expert_in[some, :] = layer_norm(sums[some, :], gain2).astype(jnp.bfloat16)
 
     def dispatch(base, count, known):
         pick = one_hot((base + slot_row[:count]) == sorted_place[:, pl.ds(0, known)])
@@ -323,32 +414,78 @@
                 recv[slots_of(0), :] = buf[slots_of(0), :]
 
     pieces = tokens // EARLY
+    parts = [(0, FEW), (FEW, FEW)] + [(piece * EARLY, EARLY) for piece in range(1, pieces)]
     load_q.wait()
-    gather(0)
-    project_q(0, EARLY)
-    finish(0)
+    gather(0, FEW)
+    project_q(0, FEW)
+    finish(0, FEW)
     pl.semaphore_wait(barrier, size)
     base = near * cap
-    dispatch(base, 128, EARLY)
+    dispatch(base, FEW, FEW)
     load_in.start()
     load_out.start()
-    for piece in range(1, pieces):
-        gather(piece)
+    gather(FEW, FEW)
+    project_q(FEW, FEW)
+    finish(FEW, FEW)
+    dispatch(base + FEW, FEW, 2 * FEW)
+    gather(EARLY, EARLY)
+    project_q(EARLY, EARLY)
+    finish(EARLY, EARLY)
+    dispatch(base + EARLY, EARLY, 2 * EARLY)
+    for first, rows in parts[3:]:
+        gather(first, rows)
     attended[pl.ds(tokens, latents), :] = normed[pl.ds(tokens, latents), :]
-    project_q(EARLY, row_count - EARLY)
-    for piece in range(1, pieces - 1):
-        finish(piece)
-        base += 128
-        dispatch(base, 128, (piece + 1) * EARLY)
-    finish(pieces - 1)
-    for base in list(range(base + 128, slot_total, 128)) + list(range(0, near * cap, 128)):
+    attended[pl.ds(row_count, padding), :] = jnp.zeros((padding, width), jnp.bfloat16)
+    project_q(2 * EARLY, key_count - 2 * EARLY)
+    for first, rows in parts[3:-1]:
+        finish(first, rows)
+        dispatch(base + first, rows, first + rows)
+    finish(*parts[-1])
+    base += parts[-1][0]
+    for base in list(range(base, slot_total, 128)) + list(range(0, near * cap, 128)):
         count = min(128, slot_total - base, near * cap - base if base < near * cap else 128)
         dispatch(base, count, tokens)
 
+    groups = 4 if size % 4 == 0 else 1
+    steps_per = size // groups
+    group_rows = steps_per * cap
+    tiles = w_in.shape[1] // tile
+    for turn, g in enumerate([1, 0, 2, 3] if groups == 4 else [0]):
+        for step in range(g * steps_per, (g + 1) * steps_per):
+            if step:
+                sends[step].wait_recv()
+        if turn == 0:
+            load_in.wait()
+            load_out.wait()
+        here = pl.ds(g * group_rows, group_rows)
+
+        def hidden(t):
+            cols = pl.ds(pl.multiple_of(t * tile, tile), tile)
+            return gelu(matmul(recv[here, :], w_in[:, cols])).astype(jnp.bfloat16)
+
+        def project(t, slot):
+            cols = pl.ds(pl.multiple_of(t * tile, tile), tile)
+            return matmul(act[slot], w_out[cols, :])
+
+        act[0] = hidden(0)
+        acc[...] = jnp.zeros_like(acc)
+
+        def body(t, carry):
+            acc[...] += project(t - 1, (t + 1) % 2)
+            act[t % 2] = hidden(t)
+            return carry
+
+        lax.fori_loop(1, tiles, body, 0)
+        res[here, :] = (acc[...] + project(tiles - 1, (tiles - 1) % 2)).astype(jnp.bfloat16)
+        for step in range(g * steps_per, (g + 1) * steps_per):
+            if step:
+                backs[step].start()
+            else:
+                back[slots_of(0), :] = res[slots_of(0), :]
+
     tail = pl.ds(tokens, latents)
-    tail_clip = lax.broadcasted_iota(jnp.int32, (latents, 1), 0) // per_clip
-    bias[tail, :] = jnp.where(tail_clip.astype(jnp.float32) == clip_row, 0.0, -jnp.inf)
-    attend(tail, latents)
+    mask(latent_clip.astype(jnp.float32))
+    attend(tokens)
     my_latent[...] = rows_ref[tail, :].astype(jnp.float32) + matmul(attended[tail, :], w_proj[...])
     latent_copy = pltpu.make_async_remote_copy(
         src_ref=my_latent,
@@ -389,7 +526,7 @@
 
         def restore(i, carry):
             cols = pl.ds(pl.multiple_of(i * step_cols, 128), step_cols)
-            first, rest = split(acc[:, cols])
+            first, rest = split(sums[:, cols])
             second, rest = split(rest)
             third, _ = split(rest)
             mid[here, cols] = (matmul(pick, first) + matmul(pick, second)) + matmul(pick, third)
@@ -397,60 +534,24 @@
 
         lax.fori_loop(0, width // step_cols, restore, 0)
 
-    groups = 2 if size % 4 == 0 else 1
-    steps_per = size // groups
-    group_rows = steps_per * cap
-    tiles = w_in.shape[1] // tile
-    for g in range(groups):
-        for step in range(g * steps_per, (g + 1) * steps_per):
-            if step:
-                sends[step].wait_recv()
-        if g == 0:
-            load_in.wait()
-            load_out.wait()
-        here = pl.ds(g * group_rows, group_rows)
-
-        def hidden(t):
-            cols = pl.ds(pl.multiple_of(t * tile, tile), tile)
-            return gelu(matmul(recv[here, :], w_in[:, cols])).astype(jnp.bfloat16)
-
-        def project(t, slot):
-            cols = pl.ds(pl.multiple_of(t * tile, tile), tile)
-            return matmul(act[slot], w_out[cols, :])
-
-        act[0] = hidden(0)
-        acc[...] = jnp.zeros_like(acc)
-
-        def body(t, carry):
-            acc[...] += project(t - 1, (t + 1) % 2)
-            act[t % 2] = hidden(t)
-            return carry
-
-        lax.fori_loop(1, tiles, body, 0)
-        res[here, :] = (acc[...] + project(tiles - 1, (tiles - 1) % 2)).astype(jnp.bfloat16)
-        for step in range(g * steps_per, (g + 1) * steps_per):
-            if step:
-                backs[step].start()
-            else:
-                back[slots_of(0), :] = res[slots_of(0), :]
-
     latent_copy.wait()
     mean = (my_latent[...] + peer_latent[...]) * 0.5
     for clip in range(clips):
         mean_ref[clip] = mean[clip * per_clip : (clip + 1) * per_clip, :].astype(jnp.bfloat16)
 
-    for g in range(groups):
-        for step in range(g * steps_per, (g + 1) * steps_per):
+    cuts = [0, size // 2, size - size // 4, size] if size % 4 == 0 else [0, size]
+    for first, last in zip(cuts[:-1], cuts[1:]):
+        for step in range(first, last):
             if step:
                 backs[step].wait_recv()
+        some = pl.ds(first * cap, (last - first) * cap)
 
         def combine(i, carry):
             here = pl.ds(pl.multiple_of(i * 128, 128), 128)
-            slot = lax.broadcasted_iota(jnp.int32, (1, group_rows), 1) + g * group_rows
+            slot = lax.broadcasted_iota(jnp.int32, (1, (last - first) * cap), 1) + first * cap
             pick = one_hot(places[here, 0:1] == slot)
-            returned = matmul(pick, back[pl.ds(g * group_rows, group_rows), :])
-            mixed = mid[here, :] + gates[here, 0:1] * returned
-            if g == groups - 1:
+            mixed = mid[here, :] + gates[here, 0:1] * matmul(pick, back[some, :])
+            if last == size:
                 out_ref[here, :] = mixed.astype(jnp.bfloat16)
             else:
                 mid[here, :] = mixed
@@ -472,7 +573,7 @@
     keys = count + 128
     cap = CAP_FACTOR * count // size
     slots = size * cap
-    groups = 2 if size % 4 == 0 else 1
+    groups = 4 if size % 4 == 0 else 1
     tile = 1024
     vmem = pl.BlockSpec(memory_space=pltpu.VMEM)
     hbm = pl.BlockSpec(memory_space=pl.ANY)
@@ -481,36 +582,48 @@
     return pl.pallas_call(
         functools.partial(layer_kernel, size, cap, tile),
         out_shape=(
-            jax.ShapeDtypeStruct((count, width), bf16),
-            jax.ShapeDtypeStruct(bottleneck.shape, bf16),
+            pltpu.VMEM((count, width), bf16),
+            pltpu.VMEM(bottleneck.shape, bf16),
         ),
-        in_specs=[hbm] + [vmem] * 7 + [hbm] * 4,
+        in_specs=[hbm] * 12,
         out_specs=(vmem, vmem),
         scratch_shapes=[
+            pltpu.VMEM(bottleneck.shape, bf16),
+            pltpu.VMEM(clip.shape, jnp.int32),
+            pltpu.VMEM(expert.shape, jnp.int32),
+            pltpu.VMEM(slot.shape, jnp.int32),
+            pltpu.VMEM(gain1.shape, bf16),
+            pltpu.VMEM(gain2.shape, bf16),
+            pltpu.VMEM(router.shape, bf16),
             pltpu.VMEM((rows, width), bf16),
             pltpu.VMEM((rows, width), bf16),
             pltpu.VMEM((width, 3 * width), bf16),
             pltpu.VMEM((width, width), bf16),
             pltpu.VMEM((width, hidden_width), bf16),
             pltpu.VMEM((hidden_width, width), bf16),
-            pltpu.VMEM((keys, 2 * width), bf16),
-            pltpu.VMEM((rows, width), bf16),
-            pltpu.VMEM((rows, width), bf16),
-            pltpu.VMEM((rows, keys), f32),
+            pltpu.VMEM((keys, width), bf16),
+            pltpu.VMEM((width, keys), bf16),
+            pltpu.VMEM((keys, 128), f32),
+            pltpu.VMEM((keys, width), bf16),
+            pltpu.VMEM((keys, width), bf16),
+            pltpu.VMEM((keys, EARLY), f32),
             pltpu.VMEM((count, width), f32),
             pltpu.VMEM((count, width), bf16),
             pltpu.VMEM((count, 128), f32),
             pltpu.VMEM((count, 128), jnp.int32),
             pltpu.VMEM((1, count), jnp.int32),
+            pltpu.VMEM((1, count), f32),
             pltpu.VMEM((slots, width), bf16),
             pltpu.VMEM((slots, width), bf16),
             pltpu.VMEM((slots, width), bf16),
             pltpu.VMEM((slots, width), bf16),
             pltpu.VMEM((slots // groups, width), f32),
             pltpu.VMEM((2, slots // groups, tile), bf16),
+            pltpu.VMEM((count, width), f32),
             pltpu.VMEM((latents, width), f32),
             pltpu.VMEM((latents, width), f32),
             dma(()),
+            dma((7,)),
             dma((3,)),
             dma((3,)),
             dma((2,)),

time: 121 us -> 114 us (0.942); the launches traced: 121 us -> 112 us
  Pallas kernels: 117 us -> 110 us
  local copies, waits for them, and re-layouts: 3.65 us -> 1.59 us
    pallas_call x1, Pallas kernels: 117 us -> 110 us  [layer(): pl.pallas_call(functools.partial(layer_kernel, size, cap, tile), out_shap...]
    unnamed x2, local copies, waits for them, and re-layouts: 3.65 us -> 1.59 us
where the time goes in v2:
time: 114 us; the launch traced here: 112 us
  Pallas kernels  110 us (96%)
  local copies, waits for them, and re-layouts  1.59 us (1%)
    pallas_call x1, Pallas kernels, layer(): pl.pallas_call(functools.partial(layer_kernel, size, cap, tile), out_shap...  110 us

profile of v2, /device:TPU:9, one launch (start us, length us, event | category | flops | bytes accessed | tf_op | source)
XLA Modules:
  0.0 111.8 jit_solution(8472279856988104981)
XLA Ops:
  0.6 109.5 %shard_map.131 = (bf16[512,1024]{1,0:T(8,128)(2,1)S(1)}, bf16[4,4,1024]{2,1,0:T(4,128)(2,1)S(1)}) custom-call(bf16[512,1024]{1,0:T(8,128)(2,1)} %bitcast.12, bf16[4,4,1024]{2,1,0:T(4,128)(2,1)} %latent_hbm.1, s32[1,512]{1,0:T(1,128)} %clip_hbm.1, s32[1,512]{1,0:T(1,128)} %expert_hbm.1, s32[1,512]{1,0:T(1,128)} %slot_hbm.1, bf16[1,1024]{1,0:T(2,128)(2,1)} %gain1_hbm.1, ...), custom_call_target="tpu_custom_call" | custom-call | tf_op jit(solution)/shard_map/pallas_call | solution.py:582
  110.2 1.0 copy.16
  111.2 0.6 copy.17

commit v3 on v2

--- a/solution.py
+++ b/solution.py
@@ -112,7 +112,9 @@
     mod = lax.axis_index("mod")
     high, low = me // near, me % near
     shifts = [0] + sorted(range(1, far), key=lambda s: (abs(2 * s - far), s))
-    order = [(s, d) for s in shifts for d in range(near)]
+    order = [(s, d) for s in shifts[:2] for d in range(near)]
+    for index in range(2, far, 2):
+        order += [(s, d) for d in range(near) for s in shifts[index : index + 2]]
 
     def ahead(step):
         s, d = order[step]

time: 114 us -> 111 us (0.974); the launches traced: 112 us -> 111 us
  Pallas kernels: 110 us -> 108 us
where the time goes in v3:
time: 111 us
  Pallas kernels  108 us (97%)
  local copies, waits for them, and re-layouts  1.59 us (1%)
    pallas_call x1, Pallas kernels, layer(): pl.pallas_call(functools.partial(layer_kernel, size, cap, tile), out_shap...  108 us

profile of v3, /device:TPU:9, one launch (start us, length us, event | category | flops | bytes accessed | tf_op | source)
XLA Modules:
  0.0 110.7 jit_solution(12799320420146522261)
XLA Ops:
  0.6 108.4 %shard_map.131 = (bf16[512,1024]{1,0:T(8,128)(2,1)S(1)}, bf16[4,4,1024]{2,1,0:T(4,128)(2,1)S(1)}) custom-call(bf16[512,1024]{1,0:T(8,128)(2,1)} %bitcast.12, bf16[4,4,1024]{2,1,0:T(4,128)(2,1)} %latent_hbm.1, s32[1,512]{1,0:T(1,128)} %clip_hbm.1, s32[1,512]{1,0:T(1,128)} %expert_hbm.1, s32[1,512]{1,0:T(1,128)} %slot_hbm.1, bf16[1,1024]{1,0:T(2,128)(2,1)} %gain1_hbm.1, ...), custom_call_target="tpu_custom_call" | custom-call | tf_op jit(solution)/shard_map/pallas_call | solution.py:584
  109.1 1.0 copy.16
  110.1 0.6 copy.17
